TPU v7x, 32 devices: a whole 2x2x4 slice. The times are simulated.
32 devices in a mesh: replica: 8 (over y, x, core), mp: 4 (over z).
Axes of the slice: x: 2, y: 2, z: 4, core: 2. Of those that a mesh axis runs over, the one named last changes fastest.
Arguments:
- pseudo_grad: bfloat16 [8, 2, 3072, 2048], P('replica', None, None, 'mp'), may hold values from -6 to 6
- outer_params: float32 [2, 3072, 2048], P(None, 'replica', 'mp'), may hold values from -6 to 6
- momentum: float32 [2, 3072, 2048], P(None, 'replica', 'mp'), may hold values from -3 to 3
- acts: bfloat16 [1024, 3072], P('replica', 'mp'), may hold values from -6 to 6
- queries: bfloat16 [1024, 2048], P('replica', 'mp'), may hold values from -6 to 6
- keys: bfloat16 [1024, 2048], P('replica', 'mp'), may hold values from -6 to 6
- doc_ids: int32 [1024], P('replica'), may hold values from 0 to 31, never falling along the last dimension, each value on 1 to 64 neighbouring positions
Outputs:
- new_outer: float32 [2, 3072, 2048], P(None, 'replica', 'mp')
- new_momentum: float32 [2, 3072, 2048], P(None, 'replica', 'mp')
- new_local: bfloat16 [8, 3072, 2048], P('replica', None, 'mp')
Inputs may be any that keep to these rules, and one draw needn't show every extreme that they name: doc_ids never fall along the rows; each document covers 1 to 64 positions.
All inputs are finite; a program needn't handle non-finite values.
Results may differ from a plain program's by a relative error of at most 0.0037.
The roundings to bfloat16 on the way count: a program that leaves them out, or rounds other values in their place, can miss the bound.
Values may be sent and summed in bfloat16 or wider, within the bound.
A program may use at most 64 MiB of HBM per device.

v0:
```python
import jax
import jax.numpy as jnp
from jax import lax
from jax.sharding import PartitionSpec as P

HD = 256
norm_eps = 1e-06
outer_rate = 0.7
outer_beta = 0.9
inner_rate = 0.1


def attend(query, key_rows, value_rows, doc_rows):
    count = query.shape[0]
    scores = jnp.einsum(
        "qhd,khd->hqk", query, key_rows, preferred_element_type=jnp.float32
    ) * query.shape[2] ** (-0.5)
    row_pos = lax.broadcasted_iota(jnp.int32, (count, count), 0)
    col_pos = lax.broadcasted_iota(jnp.int32, (count, count), 1)
    allowed = (row_pos >= col_pos) & (doc_rows[:, None] == doc_rows[None, :])
    scores = jnp.where(allowed[None], scores, -1e30)
    probs = jax.nn.softmax(scores, axis=-1).astype(jnp.bfloat16)
    context = jnp.einsum("hqk,khd->qhd", probs, value_rows, preferred_element_type=jnp.float32)
    return context.astype(jnp.bfloat16)


def outer_update(summed, params_rows, moment_rows, workers):
    delta = summed / workers
    moment_next = outer_beta * moment_rows + delta
    params_next = params_rows - outer_rate * (delta + outer_beta * moment_next)
    return (params_next, moment_next)


def shards(pseudo_grad, outer_params, momentum, acts, queries, keys, doc_ids):
    workers = lax.axis_size("replica")
    groups = lax.axis_size("mp")
    full_x = lax.all_gather(acts, "mp", axis=1, tiled=True)
    blocks = lax.all_to_all(pseudo_grad, "replica", split_axis=2, concat_axis=0, tiled=True)
    summed = jnp.sum(blocks.astype(jnp.float32), axis=0)
    new_outer, new_momentum = outer_update(summed, outer_params, momentum, workers)
    weights = lax.all_gather(new_outer.astype(jnp.bfloat16), "replica", axis=1, tiled=True)
    count, width = full_x.shape
    cols = weights.shape[2]
    heads_here = cols // HD
    all_cols = cols * groups
    rows_f = full_x.astype(jnp.float32)
    normed = (
        rows_f * lax.rsqrt(jnp.mean(rows_f * rows_f, axis=-1, keepdims=True) + norm_eps)
    ).astype(jnp.bfloat16)
    values = (
        jnp.dot(normed, weights[0], preferred_element_type=jnp.float32) * width ** (-0.5)
    ).astype(jnp.bfloat16)
    query = queries.reshape(count, heads_here, HD)
    keyed = keys.reshape(count, heads_here, HD)

    def attn_fn(c):
        return attend(query, keyed, c, doc_ids)

    context, pullback = jax.vjp(attn_fn, values.reshape(count, heads_here, HD))
    ctx = context.reshape(count, cols)
    partial_branch = lax.dot_general(
        ctx, weights[1], (((1,), (1,)), ((), ())), preferred_element_type=jnp.float32
    ) * all_cols ** (-0.5)
    branch = lax.psum(partial_branch.astype(jnp.bfloat16), "mp").astype(jnp.float32)
    dout = (rows_f + branch - jnp.roll(rows_f, -1, axis=0)).astype(jnp.bfloat16)
    dctx = (
        jnp.dot(dout, weights[1], preferred_element_type=jnp.float32) * all_cols ** (-0.5)
    ).astype(jnp.bfloat16)
    pulled = pullback(dctx.reshape(count, heads_here, HD))[0]
    grad = lax.dot_general(
        normed,
        pulled.reshape(count, cols),
        (((0,), (0,)), ((), ())),
        preferred_element_type=jnp.float32,
    ) * width ** (-0.5)
    squares = lax.psum(jnp.sum(grad * grad), "mp")
    rms = jnp.sqrt(squares / (width * all_cols) + norm_eps)
    new_local = (weights[0].astype(jnp.float32) - inner_rate * grad / rms).astype(jnp.bfloat16)
    return (new_outer, new_momentum, new_local[None])


def solution(mesh):
    placed = (
        P("replica", None, None, "mp"),
        P(None, "replica", "mp"),
        P(None, "replica", "mp"),
        P("replica", "mp"),
        P("replica", "mp"),
        P("replica", "mp"),
        P("replica"),
    )
    return jax.shard_map(
        shards,
        mesh=mesh,
        in_specs=placed,
        out_specs=(P(None, "replica", "mp"), P(None, "replica", "mp"), P("replica", None, "mp")),
        check_vma=False,
    )
```

profile of v0, /device:TPU:0, one launch (start us, length us, event | category | flops | bytes accessed | tf_op | source)
XLA Modules:
  0.0 232.5 jit_solution(10670747100160510871)
XLA Ops:
  7.2 0.0 all-gather.2.cloned.1.call-start
  7.2 11.1 %copy.23 = bf16[1,2,3072,512]{3,1,0,2:T(2,128)(2,1)S(1)} copy(bf16[1,2,3072,512]{3,2,1,0:T(8,128)(2,1)} %param.7) | data formatting | bytes 12582912 | tf_op args[0]
  18.3 76.5 %all_to_all.4 = bf16[1,2,3072,512]{3,1,0,2:T(2,128)(2,1)S(1)} all-to-all(bf16[1,2,3072,512]{3,1,0,2:T(2,128)(2,1)S(1)} %copy.23), channel_id=1, replica_groups=mesh['replica'=8,'mp'=4] {'replica'}, dimensions={2} | all-to-all | bytes 12582912 | tf_op jit(solution)/shard_map/all_to_all | solution.py:38
  94.8 6.3 %convert_reduce_fusion = f32[2,384,512]{2,0,1:T(2,128)S(1)} fusion(bf16[2,8,384,512]{3,0,2,1:T(2,128)(2,1)S(1)} %bitcast.46), kind=kLoop, calls=%fused_computation.1 | loop fusion | flops 5898240 | bytes 7864320 | tf_op jit(solution)/shard_map/reduce_sum | solution.py:39
  101.1 0.0 copy-done
  101.1 0.0 copy-start.3
  101.1 0.0 copy-start.4
  101.1 0.0 copy-start.5
  101.1 0.0 copy-start.2
  101.1 2.7 %fusion.21 = (bf16[2,384,512]{2,1,0:T(8,128)(2,1)}, f32[2,384,512]{2,1,0:T(8,128)}, f32[2,384,512]{2,1,0:T(8,128)}) fusion(f32[2,384,512]{2,1,0:T(8,128)S(1)} %copy-done, f32[2,384,512]{2,0,1:T(2,128)S(1)} %convert_reduce_fusion, f32[2,384,512]{2,1,0:T(8,128)S(1)} %copy-done.1), kind=kLoop, calls=%fused_computation.38 | loop fusion | flops 3145728 | bytes 8650752 | tf_op jit(solution)/shard_map/convert_element_type | solution.py:41
  103.8 0.0 all-gather.2.cloned.1.call-update
  103.8 0.0 all-reduce.2.cloned.1.call-start
  103.9 0.1 fusion.19
  104.0 0.2 fusion.12
  104.2 0.1 fusion.22
  104.3 0.0 copy-done.2
  104.3 19.8 %all_gather.7 = bf16[128,3072]{1,0:T(8,128)(2,1)S(1)} all-gather(bf16[128,768]{1,0:T(8,128)(2,1)S(1)} %copy-done.2), channel_id=1, replica_groups=mesh['replica'=8,'mp'=4] {'mp'}, dimensions={1}, use_global_device_ids=true | all-gather | bytes 983040 | tf_op jit(solution)/shard_map/all_gather | solution.py:37
  124.1 0.2 multiply_reduce_fusion.1
  124.3 24.4 %all-gather.2.cloned.1.call-done = bf16[2,3072,512]{2,1,0:T(8,128)(2,1)} async-done(((bf16[2,384,512]{2,1,0:T(8,128)(2,1)}), bf16[2,3072,512]{2,1,0:T(8,128)(2,1)}) %all-gather.2.cloned.1.call-update) | async-done | bytes 6291472 | tf_op jit(solution)/shard_map/all_gather | solution.py:41
  148.7 2.5 %fusion.9 = bf16[128,512]{1,0:T(8,128)(2,1)S(1)} fusion(bf16[2,3072,512]{2,1,0:T(8,128)(2,1)} %all-gather.2.cloned.1.call-done, bf16[128,3072]{1,0:T(8,128)(2,1)S(1)} %all_gather.7, f32[128]{0:T(128)S(1)} %add_rsqrt_fusion), kind=kOutput, calls=%fused_computation.23 | convolution fusion | flops 403963904 | bytes 4063744 | tf_op jit(solution)/shard_map/dot_general | solution.py:51
  151.3 0.1 copy.33
  151.4 0.2 convolution_convert_fusion.1
  151.6 3.9 %fusion.1 = bf16[128,3072]{1,0:T(8,128)(2,1)} fusion(bf16[128,512]{0,1:T(8,128)(2,1)S(1)} %bitcast.52, bf16[2,3072,512]{2,1,0:T(8,128)(2,1)} %all-gather.2.cloned.1.call-done), kind=kOutput, calls=%fused_computation.5 | convolution fusion | flops 403439616 | bytes 4063232 | tf_op jit(solution)/shard_map/dot_general | solution.py:61
  155.5 0.0 all-reduce.2.cloned.1.call-update
  155.6 0.2 slice.22
  155.8 43.8 %all-reduce.2.cloned.1.call-done = bf16[128,3072]{1,0:T(8,128)(2,1)} async-done(((bf16[128,3072]{1,0:T(8,128)(2,1)}), bf16[128,3072]{1,0:T(8,128)(2,1)}) %all-reduce.2.cloned.1.call-update) | async-done | bytes 786448 | tf_op jit(solution)/shard_map/psum | solution.py:64
  199.6 2.8 %fusion.10 = bf16[128,512]{1,0:T(8,128)(2,1)S(1)} fusion(bf16[2,3072,512]{2,1,0:T(8,128)(2,1)} %all-gather.2.cloned.1.call-done, f32[1,3072]{1,0:T(1,128)S(1)} %slice.23, f32[127,3072]{1,0:T(8,128)S(1)} %slice.22, bf16[128,3072]{1,0:T(8,128)(2,1)} %all-reduce.2.cloned.1.call-done, bf16[128,3072]{1,0:T(8,128)(2,1)S(1)} %all_gather.7), kind=kOutput, calls=%fused_computation.24 | convolution fusion | flops 405143552 | bytes 6422528 | tf_op jit(solution)/shard_map/dot_general | solution.py:67
  202.4 0.1 copy.34
  202.5 0.2 convolution_convert_fusion
  202.7 5.1 %multiply_reduce_fusion = (f32[]{:T(128)}, f32[3072,512]{1,0:T(8,128)}) fusion(bf16[128,512]{0,1:T(8,128)(2,1)S(1)} %bitcast.47, bf16[128,3072]{1,0:T(8,128)(2,1)S(1)} %all_gather.7, f32[128]{0:T(128)S(1)} %add_rsqrt_fusion), kind=kOutput, calls=%fused_computation.3 | convolution fusion | flops 408551424 | bytes 7209476 | tf_op jit(solution)/shard_map/dot_general | solution.py:70
  207.8 10.6 %psum.15 = f32[]{:T(128)} all-reduce(f32[]{:T(128)} %get-tuple-element.6), channel_id=1, replica_groups=mesh['replica'=8,'mp'=4] {'mp'}, use_global_device_ids=true, to_apply=%region_6.7 | all-reduce | flops 1 | bytes 8 | tf_op jit(solution)/shard_map/psum | solution.py:76
  219.1 6.5 %fusion.2 = bf16[1,3072,512]{2,1,0:T(8,128)(2,1)} fusion(f32[]{:T(128)S(6)} %sqrt.3, f32[3072,512]{1,0:T(8,128)} %get-tuple-element.7, bf16[2,3072,512]{2,1,0:T(8,128)(2,1)} %all-gather.2.cloned.1.call-done), kind=kLoop, calls=%fused_computation.8 | loop fusion | flops 7864320 | bytes 12582916 | tf_op jit(solution)/shard_map/broadcast_in_dim | solution.py:79
  (8 shorter events, 0.0 us)
Async XLA Ops:
  7.2 141.6 %all-gather.2.cloned.1.call-start = ((), (), s32[]{:S(2)}) async-start(), calls=%async_computation.1 | async-start | bytes 7077888 | tf_op jit(solution)/shard_map/all_gather | solution.py:41
  94.8 6.3 %copy-start = (f32[2,384,512]{2,1,0:T(8,128)S(1)}, f32[2,384,512]{2,1,0:T(8,128)}, u32[]{:S(2)}) copy-start(f32[2,384,512]{2,1,0:T(8,128)} %param.8) | copy-start | bytes 4718596
  94.8 6.3 %copy-start.1 = (f32[2,384,512]{2,1,0:T(8,128)S(1)}, f32[2,384,512]{2,1,0:T(8,128)}, u32[]{:S(2)}) copy-start(f32[2,384,512]{2,1,0:T(8,128)} %param.9) | copy-start | bytes 4718596
  101.1 2.8 %copy-start.3 = (s32[128]{0:T(128)S(1)}, s32[128]{0:T(128)}, u32[]{:S(2)}) copy-start(s32[128]{0:T(128)} %param.13) | copy-start | bytes 1540
  101.1 2.9 %copy-start.4 = (bf16[128,512]{1,0:T(8,128)(2,1)S(1)}, bf16[128,512]{1,0:T(8,128)(2,1)}, u32[]{:S(2)}) copy-start(bf16[128,512]{1,0:T(8,128)(2,1)} %param.12) | copy-start | bytes 393220
  101.1 2.9 %copy-start.5 = (bf16[128,512]{1,0:T(8,128)(2,1)S(1)}, bf16[128,512]{1,0:T(8,128)(2,1)}, u32[]{:S(2)}) copy-start(bf16[128,512]{1,0:T(8,128)(2,1)} %param.11) | copy-start | bytes 393220
  101.1 3.1 %copy-start.2 = (bf16[128,768]{1,0:T(8,128)(2,1)S(1)}, bf16[128,768]{1,0:T(8,128)(2,1)}, u32[]{:S(2)}) copy-start(bf16[128,768]{1,0:T(8,128)(2,1)} %param.10) | copy-start | bytes 589828
  103.8 95.7 %all-reduce.2.cloned.1.call-start = ((), (), s32[]{:S(2)}) async-start(), calls=%async_computation.2 | async-start | bytes 1572864 | tf_op jit(solution)/shard_map/psum | solution.py:64
Sparse Core Ops, SparseCore 0:
  103.9 44.7 all-gather.1
  155.7 43.8 all-reduce.1
where the time goes:
time: 233 us; the launch traced here: 232 us
  blocking collectives  107 us (46%)
  waiting for transfers between devices  68.2 us (29%)
  other arithmetic  15.8 us (7%)
  matrix products  15 us (6%)
  between operations  14.9 us (6%)
  local copies, waits for them, and re-layouts  11.6 us (5%)
    all_to_all x1, blocking collectives, shards(): lax.all_to_all(pseudo_grad, 'replica', split_axis=2, concat_axis=0, tiled...  76.5 us
    psum x1, waiting for transfers between devices, shards(): lax.psum(partial_branch.astype(jnp.bfloat16), 'mp').astype(jnp.float32)  43.8 us
    all_gather x1, waiting for transfers between devices, shards(): lax.all_gather(new_outer.astype(jnp.bfloat16), 'replica', axis=1, tiled=T...  24.4 us
    all_gather x1, blocking collectives, shards(): full_x = lax.all_gather(acts, 'mp', axis=1, tiled=True)  19.8 us
    unnamed x13, local copies, waits for them, and re-layouts  11.1 us
    psum x1, blocking collectives, shards(): squares = lax.psum(jnp.sum(grad * grad), 'mp')  10.6 us
    broadcast_in_dim x1, other arithmetic, shards(): return (new_outer, new_momentum, new_local[None])  6.48 us
    reduce_sum x1, other arithmetic, shards(): summed = jnp.sum(blocks.astype(jnp.float32), axis=0)  6.26 us
  transfers between devices with their start and end apart: 2, of which 2 were waited for; matrix products, arithmetic and copies ran while one was open for 0% of the time, Pallas kernels for 0%

commit v1 on v0

--- a/solution.py
+++ b/solution.py
@@ -8,6 +8,11 @@
 outer_rate = 0.7
 outer_beta = 0.9
 inner_rate = 0.1
+
+
+def add_all(x, axis):
+    blocks = lax.all_gather(x, axis)
+    return jnp.sum(blocks, axis=0)
 
 
 def attend(query, key_rows, value_rows, doc_rows):
@@ -61,7 +66,7 @@
     partial_branch = lax.dot_general(
         ctx, weights[1], (((1,), (1,)), ((), ())), preferred_element_type=jnp.float32
     ) * all_cols ** (-0.5)
-    branch = lax.psum(partial_branch.astype(jnp.bfloat16), "mp").astype(jnp.float32)
+    branch = add_all(partial_branch.astype(jnp.bfloat16), "mp").astype(jnp.float32)
     dout = (rows_f + branch - jnp.roll(rows_f, -1, axis=0)).astype(jnp.bfloat16)
     dctx = (
         jnp.dot(dout, weights[1], preferred_element_type=jnp.float32) * all_cols ** (-0.5)

time: 233 us -> 254 us (1.090)
  waiting for transfers between devices: 68.2 us -> 87.8 us
    all_gather x0 -> x1, waiting for transfers between devices: none -> 63.4 us  [add_all(): blocks = lax.all_gather(x, axis)]
    psum x1 -> x0, waiting for transfers between devices: 43.8 us -> none  [shards(): lax.psum(partial_branch.astype(jnp.bfloat16), 'mp').astype(jnp.float32)]
where the time goes in v1:
time: 254 us; the launch traced here: 253 us
  blocking collectives  106 us (42%)
  waiting for transfers between devices  87.8 us (35%)
  other arithmetic  18.3 us (7%)
  between operations  14.9 us (6%)
  matrix products  14.6 us (6%)
  local copies, waits for them, and re-layouts  11.6 us (5%)
    all_to_all x1, blocking collectives, shards(): lax.all_to_all(pseudo_grad, 'replica', split_axis=2, concat_axis=0, tiled...  76.5 us
    all_gather x1, waiting for transfers between devices, add_all(): blocks = lax.all_gather(x, axis)  63.4 us
    all_gather x1, waiting for transfers between devices, shards(): lax.all_gather(new_outer.astype(jnp.bfloat16), 'replica', axis=1, tiled=T...  24.4 us
    all_gather x1, blocking collectives, shards(): full_x = lax.all_gather(acts, 'mp', axis=1, tiled=True)  19.8 us
    unnamed x13, local copies, waits for them, and re-layouts  11.1 us
    psum x1, blocking collectives, shards(): squares = lax.psum(jnp.sum(grad * grad), 'mp')  9.7 us
    broadcast_in_dim x1, other arithmetic, shards(): return (new_outer, new_momentum, new_local[None])  6.48 us
    reduce_sum x1, other arithmetic, shards(): summed = jnp.sum(blocks.astype(jnp.float32), axis=0)  6.26 us
  transfers between devices with their start and end apart: 2, of which 2 were waited for; matrix products, arithmetic and copies ran while one was open for 0% of the time, Pallas kernels for 0%

profile of v1, /device:TPU:0, one launch (start us, length us, event | category | flops | bytes accessed | tf_op | source)
XLA Modules:
  0.0 253.3 jit_solution(14867964721753394341)
XLA Ops:
  7.2 0.0 all-gather.4.cloned.1.call-start
  7.2 11.1 %copy.23 = bf16[1,2,3072,512]{3,1,0,2:T(2,128)(2,1)S(1)} copy(bf16[1,2,3072,512]{3,2,1,0:T(8,128)(2,1)} %param.7) | data formatting | bytes 12582912 | tf_op args[0]
  18.3 76.5 %all_to_all.4 = bf16[1,2,3072,512]{3,1,0,2:T(2,128)(2,1)S(1)} all-to-all(bf16[1,2,3072,512]{3,1,0,2:T(2,128)(2,1)S(1)} %copy.23), channel_id=1, replica_groups=mesh['replica'=8,'mp'=4] {'replica'}, dimensions={2} | all-to-all | bytes 12582912 | tf_op jit(solution)/shard_map/all_to_all | solution.py:43
  94.8 6.3 %convert_reduce_fusion = f32[2,384,512]{2,0,1:T(2,128)S(1)} fusion(bf16[2,8,384,512]{3,0,2,1:T(2,128)(2,1)S(1)} %bitcast.47), kind=kLoop, calls=%fused_computation.1 | loop fusion | flops 5898240 | bytes 7864320 | tf_op jit(solution)/shard_map/reduce_sum | solution.py:44
  101.1 0.0 copy-start.3
  101.1 0.0 copy-start.4
  101.1 0.0 copy-start.5
  101.1 0.0 copy-start.2
  101.1 2.7 %fusion.21 = (bf16[2,384,512]{2,1,0:T(8,128)(2,1)}, f32[2,384,512]{2,1,0:T(8,128)}, f32[2,384,512]{2,1,0:T(8,128)}) fusion(f32[2,384,512]{2,1,0:T(8,128)S(1)} %copy-done, f32[2,384,512]{2,0,1:T(2,128)S(1)} %convert_reduce_fusion, f32[2,384,512]{2,1,0:T(8,128)S(1)} %copy-done.1), kind=kLoop, calls=%fused_computation.38 | loop fusion | flops 3145728 | bytes 8650752 | tf_op jit(solution)/shard_map/convert_element_type | solution.py:46
  103.8 0.0 all-gather.4.cloned.1.call-update
  103.8 0.0 all-gather.6.cloned.1.call-start
  103.9 0.1 fusion.19
  104.0 0.2 fusion.12
  104.2 0.1 fusion.22
  104.3 0.0 copy-done.2
  104.3 19.8 %all_gather.13 = bf16[128,3072]{1,0:T(8,128)(2,1)S(1)} all-gather(bf16[128,768]{1,0:T(8,128)(2,1)S(1)} %copy-done.2), channel_id=1, replica_groups=mesh['replica'=8,'mp'=4] {'mp'}, dimensions={1}, use_global_device_ids=true | all-gather | bytes 983040 | tf_op jit(solution)/shard_map/all_gather | solution.py:42
  124.1 0.2 multiply_reduce_fusion.1
  124.3 24.4 %all-gather.4.cloned.1.call-done = bf16[2,3072,512]{2,1,0:T(8,128)(2,1)} async-done(((bf16[2,384,512]{2,1,0:T(8,128)(2,1)}), bf16[2,3072,512]{2,1,0:T(8,128)(2,1)}) %all-gather.4.cloned.1.call-update) | async-done | bytes 6291472 | tf_op jit(solution)/shard_map/all_gather | solution.py:46
  148.7 2.5 fusion.9
  151.3 0.1 copy.33
  151.4 0.2 convolution_convert_fusion.1
  151.6 3.9 %fusion.1 = bf16[128,3072]{1,0:T(8,128)(2,1)} fusion(bf16[128,512]{0,1:T(8,128)(2,1)S(1)} %bitcast.54, bf16[2,3072,512]{2,1,0:T(8,128)(2,1)} %all-gather.4.cloned.1.call-done), kind=kOutput, calls=%fused_computation.5 | convolution fusion | flops 403439616 | bytes 4063232 | tf_op jit(solution)/shard_map/dot_general | solution.py:66
  155.5 0.0 all-gather.6.cloned.1.call-update
  155.6 0.2 slice.22
  155.8 63.4 %all-gather.6.cloned.1.call-done = bf16[512,3072]{1,0:T(8,128)(2,1)} async-done(((bf16[128,3072]{1,0:T(8,128)(2,1)}), bf16[512,3072]{1,0:T(8,128)(2,1)}) %all-gather.6.cloned.1.call-update) | async-done | bytes 3145744 | tf_op jit(solution)/shard_map/all_gather | solution.py:14
  219.2 2.5 reduce_sum.51
  221.7 2.5 fusion.10
  224.2 0.1 copy.34
  224.3 0.2 convolution_convert_fusion
  224.5 5.1 %multiply_reduce_fusion = (f32[]{:T(128)}, f32[3072,512]{1,0:T(8,128)}) fusion(bf16[128,512]{0,1:T(8,128)(2,1)S(1)} %bitcast.49, bf16[128,3072]{1,0:T(8,128)(2,1)S(1)} %all_gather.13, f32[128]{0:T(128)S(1)} %add_rsqrt_fusion), kind=kOutput, calls=%fused_computation.3 | convolution fusion | flops 408551424 | bytes 7209476 | tf_op jit(solution)/shard_map/dot_general | solution.py:75
  229.6 9.7 %psum.7 = f32[]{:T(128)} all-reduce(f32[]{:T(128)} %get-tuple-element.6), channel_id=1, replica_groups=mesh['replica'=8,'mp'=4] {'mp'}, use_global_device_ids=true, to_apply=%region_6.7 | all-reduce | flops 1 | bytes 8 | tf_op jit(solution)/shard_map/psum | solution.py:81
  240.0 6.5 %fusion.2 = bf16[1,3072,512]{2,1,0:T(8,128)(2,1)} fusion(f32[]{:T(128)S(6)} %sqrt.3, f32[3072,512]{1,0:T(8,128)} %get-tuple-element.7, bf16[2,3072,512]{2,1,0:T(8,128)(2,1)} %all-gather.4.cloned.1.call-done), kind=kLoop, calls=%fused_computation.8 | loop fusion | flops 7864320 | bytes 12582916 | tf_op jit(solution)/shard_map/broadcast_in_dim | solution.py:84
  (9 shorter events, 0.0 us)
Async XLA Ops:
  7.2 141.6 %all-gather.4.cloned.1.call-start = ((), (), s32[]{:S(2)}) async-start(), calls=%async_computation.1 | async-start | bytes 7077888 | tf_op jit(solution)/shard_map/all_gather | solution.py:46
  94.8 6.3 %copy-start = (f32[2,384,512]{2,1,0:T(8,128)S(1)}, f32[2,384,512]{2,1,0:T(8,128)}, u32[]{:S(2)}) copy-start(f32[2,384,512]{2,1,0:T(8,128)} %param.8) | copy-start | bytes 4718596
  94.8 6.3 %copy-start.1 = (f32[2,384,512]{2,1,0:T(8,128)S(1)}, f32[2,384,512]{2,1,0:T(8,128)}, u32[]{:S(2)}) copy-start(f32[2,384,512]{2,1,0:T(8,128)} %param.9) | copy-start | bytes 4718596
  101.1 2.8 %copy-start.3 = (s32[128]{0:T(128)S(1)}, s32[128]{0:T(128)}, u32[]{:S(2)}) copy-start(s32[128]{0:T(128)} %param.13) | copy-start | bytes 1540
  101.1 2.9 %copy-start.4 = (bf16[128,512]{1,0:T(8,128)(2,1)S(1)}, bf16[128,512]{1,0:T(8,128)(2,1)}, u32[]{:S(2)}) copy-start(bf16[128,512]{1,0:T(8,128)(2,1)} %param.12) | copy-start | bytes 393220
  101.1 2.9 %copy-start.5 = (bf16[128,512]{1,0:T(8,128)(2,1)S(1)}, bf16[128,512]{1,0:T(8,128)(2,1)}, u32[]{:S(2)}) copy-start(bf16[128,512]{1,0:T(8,128)(2,1)} %param.11) | copy-start | bytes 393220
  101.1 3.1 %copy-start.2 = (bf16[128,768]{1,0:T(8,128)(2,1)S(1)}, bf16[128,768]{1,0:T(8,128)(2,1)}, u32[]{:S(2)}) copy-start(bf16[128,768]{1,0:T(8,128)(2,1)} %param.10) | copy-start | bytes 589828
  103.8 115.3 %all-gather.6.cloned.1.call-start = ((), (), s32[]{:S(2)}) async-start(), calls=%async_computation.2 | async-start | bytes 3932160 | tf_op jit(solution)/shard_map/all_gather | solution.py:14
Sparse Core Ops, SparseCore 0:
  103.9 44.7 all-gather.3
  155.7 63.4 all-gather.5
